TPU v7x, 32 devices: a whole 2x2x4 slice. The times are simulated.
32 devices in a mesh: tp: 8 (over z, y), kv: 4 (over x, core).
Axes of the slice: x: 2, y: 2, z: 4, core: 2. Of those that a mesh axis runs over, the one named last changes fastest.
Arguments:
- hidden_in: bfloat16 [2048, 4096], P(('kv', 'tp')), may hold values from -6 to 6
- gain_attn: float32 [4096], replicated, may hold values from 0.4 to 1.6
- w_qkv: bfloat16 [4096, 32, 384], P(None, 'tp'), may hold values from -0.09375 to 0.09375
- cache_kv: bfloat16 [2, 8192, 32, 256], P(None, 'kv', 'tp'), may hold values from -110 to 110
- cache_len: int32 [2], replicated, may hold values from 128 to 8192, as said below
- w_out: bfloat16 [4096, 4096], P('tp'), may hold values from -0.1875 to 0.1875
- gain_mlp: float32 [4096], replicated, may hold values from 0.1 to 1.9
- w_gate_up: bfloat16 [4096, 2, 11008], P('kv', None, 'tp'), may hold values from -0.09375 to 0.09375
- w_down: bfloat16 [11008, 4096], P('tp', 'kv'), may hold values from -0.0546875 to 0.0546875
Outputs:
- layer_out: bfloat16 [2048, 4096], P(('kv', 'tp'))
Inputs may be any that keep to these rules, and one draw needn't show every extreme that they name: `cache_len`: every length is a multiple of 128; some sequence uses the whole cache.
All inputs are finite; a program needn't handle non-finite values.
Results may differ from a plain program's by a relative error of at most 0.019.
The roundings to bfloat16 on the way count: a program that leaves them out, or rounds other values in their place, can miss the bound.
Values may be sent and summed in bfloat16 or wider, within the bound.
A program may use at most 192 MiB of HBM per device.

v0:
```python
import math

import jax
import jax.numpy as jnp
from jax import lax
from jax.sharding import PartitionSpec as P

EPSILON = 1e-05
MASKED = -1e30


def rms_scale(values_in, gain_vector):
    widened = values_in.astype(jnp.float32)
    mean_square = jnp.mean(widened * widened, axis=-1, keepdims=True)
    return (widened * lax.rsqrt(mean_square + EPSILON) * gain_vector).astype(jnp.bfloat16)


def per_device(
    hidden_in, gain_attn, w_qkv, cache_kv, cache_len, w_out, gain_mlp, w_gate_up, w_down
):
    local_heads = w_qkv.shape[1]
    head_dim = w_qkv.shape[2] // 3
    own_rows = hidden_in.shape[0]
    block_input = lax.all_gather(hidden_in, "tp", axis=0, tiled=True)
    block_rows = block_input.shape[0]
    normed = rms_scale(block_input, gain_attn)
    flat_qkv = w_qkv.reshape(w_qkv.shape[0], local_heads * 3 * head_dim)
    packed = jnp.dot(normed, flat_qkv, preferred_element_type=jnp.float32).astype(jnp.bfloat16)
    packed = packed.reshape(block_rows, local_heads, 3 * head_dim)
    key_mine = packed[:, :, head_dim : 2 * head_dim]
    value_mine = packed[:, :, 2 * head_dim :]
    query_rows = lax.all_gather(packed[:, :, :head_dim], "kv", axis=0, tiled=True)
    seq_count = cache_kv.shape[0]
    span_len = query_rows.shape[0] // seq_count
    kv_index = lax.axis_index("kv")
    cache_rows = cache_kv.shape[1]
    cache_pos = kv_index * cache_rows + jnp.arange(cache_rows, dtype=jnp.int32)
    own_seq = (kv_index * block_rows + jnp.arange(block_rows, dtype=jnp.int32)) // span_len
    row_peaks, masses, accums = ([], [], [])
    for seq_id in range(seq_count):
        query_block = query_rows[seq_id * span_len : (seq_id + 1) * span_len]
        joined_key_rows = jnp.concatenate([cache_kv[seq_id, :, :, :head_dim], key_mine], axis=0)
        joined_value_rows = jnp.concatenate([cache_kv[seq_id, :, :, head_dim:], value_mine], axis=0)
        usable = jnp.concatenate([cache_pos < cache_len[seq_id], own_seq == seq_id])
        logit_scores = jnp.einsum(
            "qhd,khd->hqk", query_block, joined_key_rows, preferred_element_type=jnp.float32
        ) / math.sqrt(head_dim)
        logit_scores = jnp.where(usable[None, None, :], logit_scores, MASKED)
        row_peak = jnp.max(logit_scores, axis=2)
        raw_weights = jnp.where(
            usable[None, None, :], jnp.exp(logit_scores - row_peak[:, :, None]), 0.0
        )
        row_peaks.append(row_peak.T)
        masses.append(jnp.sum(raw_weights, axis=2).T)
        accums.append(
            jnp.einsum(
                "hqk,khd->qhd",
                raw_weights.astype(jnp.bfloat16),
                joined_value_rows,
                preferred_element_type=jnp.float32,
            )
        )
    peak_all = jnp.concatenate(row_peaks, axis=0)
    mass_all = jnp.concatenate(masses, axis=0)
    accum_all = jnp.concatenate(accums, axis=0)
    peak_set, mass_set, accum_set = (
        lax.all_to_all(peak_all[None], "kv", split_axis=1, concat_axis=0, tiled=True),
        lax.all_to_all(mass_all[None], "kv", split_axis=1, concat_axis=0, tiled=True),
        lax.all_to_all(accum_all[None], "kv", split_axis=1, concat_axis=0, tiled=True),
    )
    peak_best = jnp.max(peak_set, axis=0)
    scaling = jnp.exp(peak_set - peak_best[None])
    mass_own = jnp.sum(mass_set * scaling, axis=0)
    accum_own = jnp.sum(accum_set * scaling[..., None], axis=0)
    attended = (
        (accum_own / mass_own[..., None])
        .astype(jnp.bfloat16)
        .reshape(block_rows, local_heads * head_dim)
    )
    tp_index = lax.axis_index("tp")
    heads_sum = lax.psum(
        jnp.dot(attended, w_out, preferred_element_type=jnp.float32).astype(jnp.bfloat16), "tp"
    ).astype(jnp.float32)
    residual = block_input.astype(jnp.float32) + heads_sum
    mlp_in = rms_scale(residual, gain_mlp)
    residual_own = lax.dynamic_slice_in_dim(residual, tp_index * own_rows, own_rows, 0)
    gate_up = jnp.einsum(
        "td,dgf->tgf",
        mlp_in,
        lax.all_gather(w_gate_up, "kv", axis=0, tiled=True),
        preferred_element_type=jnp.float32,
    )
    activated = (jax.nn.silu(gate_up[:, 0, :]) * gate_up[:, 1, :]).astype(jnp.bfloat16)
    down_terms = jnp.dot(
        activated,
        lax.all_gather(w_down, "kv", axis=1, tiled=True),
        preferred_element_type=jnp.float32,
    )
    down_own = lax.psum_scatter(
        down_terms.astype(jnp.bfloat16), "tp", scatter_dimension=0, tiled=True
    ).astype(jnp.float32)
    return (residual_own + down_own).astype(jnp.bfloat16)


def solution(mesh):
    in_specs = (
        P(("kv", "tp"), None),
        P(),
        P(None, "tp", None),
        P(None, "kv", "tp", None),
        P(),
        P("tp", None),
        P(),
        P("kv", None, "tp"),
        P("tp", "kv"),
    )
    out_specs = P(("kv", "tp"), None)
    return jax.shard_map(
        per_device, mesh=mesh, in_specs=in_specs, out_specs=out_specs, check_vma=False
    )
```

profile of v0, /device:TPU:0, one launch (start us, length us, event | category | flops | bytes accessed | tf_op | source)
XLA Modules:
  0.0 827.7 jit_solution(16002876231132787441)
XLA Ops:
  7.3 12.4 %copy.51 = bf16[512,8,4,384]{3,1,2,0:T(8,128)(2,1)} copy(bf16[512,8,4,384]{3,2,1,0:T(4,128)(2,1)} %bitcast.50) | data formatting | bytes 25165824
  19.7 65.3 %all-gather.5.cloned.1.call-done = bf16[512,4096]{1,0:T(8,128)(2,1)} async-done(((bf16[64,4096]{1,0:T(8,128)(2,1)}), bf16[512,4096]{1,0:T(8,128)(2,1)}) %all-gather.5.cloned.1.call-update) | async-done | bytes 4194320 | tf_op jit(solution)/shard_map/all_gather | solution.py:24
  85.0 3.1 fusion.12
  88.1 11.0 %fusion.24 = bf16[512,1536]{1,0:T(8,128)(2,1)S(1)} fusion(bf16[4096,1536]{1,0:T(8,128)(2,1)} %bitcast.51, bf16[512,4096]{1,0:T(8,128)(2,1)} %all-gather.5.cloned.1.call-done, f32[4096]{0:T(1024)S(1)} %copy-done.5, f32[512]{0:T(512)S(1)} %add_rsqrt_fusion.1), kind=kOutput, calls=%fused_computation.37 | convolution fusion | flops 6451625984 | bytes 18368512 | tf_op jit(solution)/shard_map/dot_general | solution.py:28
  100.9 6.4 fusion.61
  107.4 4.4 copy.44
  111.8 2.6 copy.49
  116.3 4.1 copy_bitcast_fusion
  122.2 19.4 %fusion.1 = (f32[4,1024]{1,0:T(4,128)S(1)}, f32[4,1024,2560]{2,1,0:T(8,128)}) fusion(pred[2560]{0:T(1024)(128)(4,1)S(1)} %pad_add_fusion.1, bf16[512,4,128]{2,0,1:T(8,128)(2,1)S(1)} %copy.48, bf16[2048,4,128]{2,0,1:T(8,128)(2,1)} %get-tuple-element.26, bf16[2048,4,128]{2,0,1:T(8,128)(2,1)} %all-gather.7.cloned.1.call-done), kind=kOutput, calls=%fused_computation.5 | convolution fusion | flops 2721050624 | bytes 45632000 | tf_op jit(solution)/shard_map/qhd,khd->hqk/dot_general | solution.py:45
  141.6 19.2 %fusion.4 = f32[4,1024]{1,0:T(4,128)S(1)} fusion(f32[4,1024,2560]{2,1,0:T(8,128)} %get-tuple-element.19, f32[4,1024]{1,0:T(4,128)S(1)} %get-tuple-element.18, pred[2560]{0:T(1024)(128)(4,1)S(1)} %pad_add_fusion.1), kind=kLoop, calls=%fused_computation.8 | loop fusion | flops 52424704 | bytes 41978368 | tf_op jit(solution)/shard_map/reduce_sum | solution.py:54
  160.8 17.9 %fusion.38 = f32[1024,4,128]{0,2,1:T(8,128)} fusion(f32[4,1024,2560]{2,1,0:T(8,128)} %get-tuple-element.19, f32[4,1024]{1,0:T(4,128)S(1)} %get-tuple-element.18, pred[2560]{0:T(1024)(128)(4,1)S(1)} %pad_add_fusion.1, bf16[512,4,128]{0,2,1:T(8,128)(2,1)S(1)} %copy-done.3, bf16[2048,4,128]{0,2,1:T(8,128)(2,1)S(1)} %bitcast.59), kind=kOutput, calls=%fused_computation.51 | convolution fusion | flops 2742026240 | bytes 46680576 | tf_op jit(solution)/shard_map/hqk,khd->qhd/dot_general | solution.py:56
  178.7 19.4 %fusion = (f32[4,1024]{1,0:T(4,128)S(1)}, f32[4,1024,2560]{2,1,0:T(8,128)}) fusion(pred[2560]{0:T(1024)(128)(4,1)S(1)} %pad_add_fusion, bf16[512,4,128]{2,0,1:T(8,128)(2,1)S(1)} %copy.48, bf16[2048,4,128]{2,0,1:T(8,128)(2,1)S(1)} %get-tuple-element.27, bf16[2048,4,128]{2,0,1:T(8,128)(2,1)} %all-gather.7.cloned.1.call-done), kind=kOutput, calls=%fused_computation.4 | convolution fusion | flops 2721050624 | bytes 45632000 | tf_op jit(solution)/shard_map/qhd,khd->hqk/dot_general | solution.py:45
  198.1 19.2 %fusion.2 = f32[4,1024]{1,0:T(4,128)S(1)} fusion(f32[4,1024,2560]{2,1,0:T(8,128)} %get-tuple-element.21, f32[4,1024]{1,0:T(4,128)S(1)} %get-tuple-element.20, pred[2560]{0:T(1024)(128)(4,1)S(1)} %pad_add_fusion), kind=kLoop, calls=%fused_computation.6 | loop fusion | flops 52424704 | bytes 41978368 | tf_op jit(solution)/shard_map/reduce_sum | solution.py:54
  217.3 17.9 %fusion.35 = f32[1024,4,128]{0,2,1:T(8,128)} fusion(f32[4,1024,2560]{2,1,0:T(8,128)} %get-tuple-element.21, f32[4,1024]{1,0:T(4,128)S(1)} %get-tuple-element.20, pred[2560]{0:T(1024)(128)(4,1)S(1)} %pad_add_fusion, bf16[512,4,128]{0,2,1:T(8,128)(2,1)S(1)} %copy-done.3, bf16[2048,4,128]{0,2,1:T(8,128)(2,1)S(1)} %bitcast.58), kind=kOutput, calls=%fused_computation.50 | convolution fusion | flops 2742026240 | bytes 46680576 | tf_op jit(solution)/shard_map/hqk,khd->qhd/dot_general | solution.py:56
  236.2 9.5 %reduce.2 = f32[2048,4]{1,0:T(8,128)S(1)} reduce(f32[2048,1,4]{2,1,0:T(1,128)S(1)} %bitcast.54, f32[]{:T(128)} %broadcast.98), dimensions={1}, to_apply=%bitcast.41.reduce_sub_computation | reduce | bytes 65540
  247.1 3.3 all-to-all-start.1
  250.7 9.3 %reduce = f32[2048,4]{1,0:T(8,128)S(1)} reduce(f32[2048,1,4]{2,1,0:T(1,128)S(1)} %bitcast.55, f32[]{:T(128)} %broadcast.98), dimensions={1}, to_apply=%bitcast.43.reduce_sub_computation | reduce | bytes 65540
  261.4 3.3 all-to-all-start.2
  264.7 4.6 maximum_bitcast_fusion
  269.3 5.2 copy.37
  274.6 4.9 all-to-all-start
  285.4 42.2 %all-to-all-done = f32[1,2048,4,128]{3,2,0,1:T(4,128)} async-done(((f32[1,2048,4,128]{3,2,0,1:T(4,128)}), f32[1,2048,4,128]{3,2,0,1:T(4,128)}, u32[]{:S(2)}, u32[]{:S(2)}) %all-to-all-start) | async-done | bytes 4194336 | tf_op jit(solution)/shard_map/all_to_all | solution.py:69
  327.6 5.3 copy.41
  333.0 5.1 multiply_reduce_fusion.1
  338.2 4.5 convolution_convert_fusion.1
  344.2 155.1 %all-reduce.2.cloned.1.call-done = bf16[512,4096]{1,0:T(8,128)(2,1)} async-done(((bf16[512,4096]{1,0:T(8,128)(2,1)}), bf16[512,4096]{1,0:T(8,128)(2,1)}) %all-reduce.2.cloned.1.call-update) | async-done | bytes 4194320 | tf_op jit(solution)/shard_map/psum | solution.py:81
  499.3 9.2 %convert_add_fusion = (f32[512,4096]{1,0:T(8,128)}, f32[512]{0:T(512)S(1)}) fusion(bf16[512,4096]{1,0:T(8,128)(2,1)} %all-gather.5.cloned.1.call-done, bf16[512,4096]{1,0:T(8,128)(2,1)} %all-reduce.2.cloned.1.call-done), kind=kLoop, calls=%fused_computation.14 | loop fusion | flops 10485248 | bytes 16779264 | tf_op jit(solution)/shard_map/add | solution.py:84
  508.5 131.6 %all-gather.9.cloned.1.call-done = bf16[4096,2,1376]{0,2,1:T(8,128)(2,1)} async-done(((bf16[1024,2,1376]{0,2,1:T(8,128)(2,1)}), bf16[4096,2,1376]{0,2,1:T(8,128)(2,1)}) %all-gather.9.cloned.1.call-update) | async-done | bytes 22544400 | tf_op jit(solution)/shard_map/all_gather | solution.py:90
  640.0 20.5 %fusion.16 = f32[512,2,1376]{0,2,1:T(8,128)} fusion(bf16[4096,2,1376]{0,2,1:T(8,128)(2,1)} %all-gather.9.cloned.1.call-done, f32[4096]{0:T(1024)S(1)} %copy-done.6, f32[512]{0:T(512)S(1)} %add_rsqrt_fusion, bf16[512,4096]{1,0:T(8,128)(2,1)} %all-gather.5.cloned.1.call-done, bf16[512,4096]{1,0:T(8,128)(2,1)} %all-reduce.2.cloned.1.call-done), kind=kOutput, calls=%fused_computation.25 | convolution fusion | flops 11555307520 | bytes 36587520 | tf_op jit(solution)/shard_map/td,dgf->tgf/dot_general | solution.py:87
  660.5 55.6 %all-gather.11.cloned.1.call-done = bf16[1376,4096]{1,0:T(8,128)(2,1)} async-done(((bf16[1376,1024]{1,0:T(8,128)(2,1)}), bf16[1376,4096]{1,0:T(8,128)(2,1)}) %all-gather.11.cloned.1.call-update) | async-done | bytes 11272208 | tf_op jit(solution)/shard_map/all_gather | solution.py:96
  716.1 13.6 %convolution_convert_fusion = bf16[512,4096]{1,0:T(8,128)(2,1)} fusion(bf16[1376,4096]{1,0:T(8,128)(2,1)} %all-gather.11.cloned.1.call-done, f32[512,2,1376]{0,2,1:T(8,128)} %fusion.16), kind=kOutput, calls=%fused_computation.22 | convolution fusion | flops 5777686528 | bytes 21102592 | tf_op jit(solution)/shard_map/dot_general | solution.py:94
  729.7 88.4 %reduce-scatter.2.cloned.1.call-done = bf16[64,4096]{1,0:T(8,128)(2,1)} async-done(((bf16[512,4096]{1,0:T(8,128)(2,1)}), bf16[64,4096]{1,0:T(8,128)(2,1)}) %reduce-scatter.2.cloned.1.call-update) | async-done | bytes 524304 | tf_op jit(solution)/shard_map/reduce_scatter | solution.py:99
  (59 shorter events, 20.1 us)
Async XLA Ops:
  6.5 78.5 %all-gather.5.cloned.1.call-start = ((), (), s32[]{:S(2)}) async-start(), calls=%async_computation.4 | async-start | bytes 4718592 | tf_op jit(solution)/shard_map/all_gather | solution.py:24
  7.3 114.9 %all-gather.7.cloned.1.call-start = ((), (), s32[]{:S(2)}) async-start(), calls=%async_computation.5 | async-start | bytes 2621440 | tf_op jit(solution)/shard_map/all_gather | solution.py:32
  7.3 80.8 %copy-start.5 = (f32[4096]{0:T(1024)S(1)}, f32[4096]{0:T(1024)}, u32[]{:S(2)}) copy-start(f32[4096]{0:T(1024)} %param.10) | copy-start | bytes 49156
  107.4 7.1 copy-start.4
  141.6 19.2 %copy-start.2 = (bf16[1,2048,4,128]{1,3,2,0:T(8,128)(2,1)S(1)}, bf16[1,2048,4,128]{1,3,2,0:T(8,128)(2,1)}, u32[]{:S(2)}) copy-start(bf16[1,2048,4,128]{1,3,2,0:T(8,128)(2,1)} %copy.49) | copy-start | bytes 6291460
  141.6 19.2 %copy-start.3 = (bf16[512,4,128]{0,2,1:T(8,128)(2,1)S(1)}, bf16[512,4,128]{0,2,1:T(8,128)(2,1)}, u32[]{:S(2)}) copy-start(bf16[512,4,128]{0,2,1:T(8,128)(2,1)} %copy.45) | copy-start | bytes 1572868
  198.1 19.2 %copy-start.1 = (bf16[1,2048,4,128]{1,3,2,0:T(8,128)(2,1)S(1)}, bf16[1,2048,4,128]{1,3,2,0:T(8,128)(2,1)}, u32[]{:S(2)}) copy-start(bf16[1,2048,4,128]{1,3,2,0:T(8,128)(2,1)} %copy.44) | copy-start | bytes 6291460
  247.1 14.4 %all-to-all-start.1 = ((f32[4,1,2048]{2,1,0:T(1,128)}), f32[4,1,2048]{2,1,0:T(1,128)S(1)}, u32[]{:S(2)}, u32[]{:S(2)}) async-start(f32[4,1,2048]{2,1,0:T(1,128)} %reshape.59), calls=%async_computation.1 | async-start | bytes 65536 | tf_op jit(solution)/shard_map/all_to_all | solution.py:67
  261.4 13.2 %all-to-all-start.2 = ((f32[4,1,2048]{2,1,0:T(1,128)}), f32[4,1,2048]{2,1,0:T(1,128)S(1)}, u32[]{:S(2)}, u32[]{:S(2)}) async-start(f32[4,1,2048]{2,1,0:T(1,128)} %reshape.61), calls=%async_computation.2 | async-start | bytes 65536 | tf_op jit(solution)/shard_map/all_to_all | solution.py:68
  274.6 53.1 %all-to-all-start = ((f32[1,2048,4,128]{3,2,0,1:T(4,128)}), f32[1,2048,4,128]{3,2,0,1:T(4,128)}, u32[]{:S(2)}, u32[]{:S(2)}) async-start(f32[1,2048,4,128]{3,2,0,1:T(4,128)} %copy.37), calls=%async_computation | async-start | bytes 8388608 | tf_op jit(solution)/shard_map/all_to_all | solution.py:69
  279.4 219.9 %all-reduce.2.cloned.1.call-start = ((), (), s32[]{:S(2)}) async-start(), calls=%async_computation.6 | async-start | bytes 8388608 | tf_op jit(solution)/shard_map/psum | solution.py:81
  333.0 5.3 copy-start
  342.7 297.3 %all-gather.9.cloned.1.call-start = ((), (), s32[]{:S(2)}) async-start(), calls=%async_computation.7 | async-start | bytes 28180480 | tf_op jit(solution)/shard_map/all_gather | solution.py:90
  343.3 372.8 %all-gather.11.cloned.1.call-start = ((), (), s32[]{:S(2)}) async-start(), calls=%async_computation.8 | async-start | bytes 14090240 | tf_op jit(solution)/shard_map/all_gather | solution.py:96
  343.9 296.1 %copy-start.6 = (f32[4096]{0:T(1024)S(1)}, f32[4096]{0:T(1024)}, u32[]{:S(2)}) copy-start(f32[4096]{0:T(1024)} %param.15) | copy-start | bytes 49156
  343.9 474.2 %reduce-scatter.2.cloned.1.call-start = ((), (), s32[]{:S(2)}) async-start(), calls=%async_computation.9 | async-start | bytes 4718592 | tf_op jit(solution)/shard_map/reduce_scatter | solution.py:99
Sparse Core Ops, SparseCore 0:
  9.5 75.5 all-gather.4
  101.0 21.0 all-gather.6
  342.9 156.3 all-reduce.1
  500.7 139.2 all-gather.8
  641.4 74.6 all-gather.10
  729.8 88.2 reduce-scatter.1
where the time goes:
time: 835 us; the launch traced here: 828 us
  waiting for transfers between devices  541 us (65%)
  matrix products  124 us (15%)
  other arithmetic  84.6 us (10%)
  local copies, waits for them, and re-layouts  52.2 us (6%)
  between operations  14.2 us (2%)
  starting transfers between devices  12.1 us (1%)
    psum x1, waiting for transfers between devices, per_device(): lax.psum(jnp.dot(attended, w_out, preferred_element_type=jnp.float32).ast...  155 us
    all_gather x1, waiting for transfers between devices, per_device(): lax.all_gather(w_gate_up, 'kv', axis=0, tiled=True)  132 us
    reduce_scatter x1, waiting for transfers between devices, per_device(): lax.psum_scatter(down_terms.astype(jnp.bfloat16), 'tp', scatter_dimension...  88.4 us
    all_gather x1, waiting for transfers between devices, per_device(): block_input = lax.all_gather(hidden_in, 'tp', axis=0, tiled=True)  65.3 us
    all_gather x1, waiting for transfers between devices, per_device(): lax.all_gather(w_down, 'kv', axis=1, tiled=True)  55.6 us
    all_to_all x1, waiting for transfers between devices, per_device(): lax.all_to_all(accum_all[None], 'kv', split_axis=1, concat_axis=0, tiled=...  42.2 us
    dot_general x2, matrix products, per_device(): jnp.einsum('qhd,khd->hqk', query_block, joined_key_rows, preferred_elemen...  38.8 us
    reduce_sum x2, other arithmetic, per_device(): masses.append(jnp.sum(raw_weights, axis=2).T)  38.4 us
  transfers between devices with their start and end apart: 9, of which 7 were waited for; matrix products, arithmetic and copies ran while one was open for 11% of the time, Pallas kernels for 0%

commit v1 on v0

v1 whole, which is shorter than its diff:
```python
import functools
import math

import jax
import jax.numpy as jnp
from jax import lax
from jax.experimental import pallas as pl
from jax.experimental.pallas import tpu as pltpu
from jax.sharding import PartitionSpec as P


EPSILON = 1e-05
MASKED = -1e30
PARTS = 1


def rms_scale(values_in, gain_vector):
    widened = values_in.astype(jnp.float32)
    mean_square = jnp.mean(widened * widened, axis=-1, keepdims=True)
    return (widened * lax.rsqrt(mean_square + EPSILON) * gain_vector).astype(jnp.bfloat16)


def attention_kernel(seqs, heads, chunk, meta, q_ref, kv_ref, own_k, own_v, out_ref):
    seq, head = pl.program_id(0), pl.program_id(2)
    valid, own = meta[seq], meta[seqs + seq]
    width = q_ref.shape[1]
    rows = q_ref.shape[0]
    to_log2 = math.log2(math.e) / math.sqrt(width)
    query = q_ref[...]

    def step(keys, values, bias, carry):
        peak, mass, total = carry
        scores = lax.dot_general(
            query, keys, (((1,), (1,)), ((), ())), preferred_element_type=jnp.float32
        )
        if bias is not None:
            scores = scores + bias
        peak_new = jnp.maximum(peak, jnp.max(scores, axis=1, keepdims=True))
        weights = jnp.exp2((scores - peak_new) * to_log2)
        fade = jnp.exp2((peak - peak_new) * to_log2)
        mass = mass * fade + jnp.sum(weights, axis=1, keepdims=True)
        total = total * fade + jnp.dot(
            weights.astype(jnp.bfloat16), values, preferred_element_type=jnp.float32
        )
        return peak_new, mass, total

    def full_step(i, carry):
        at = pl.multiple_of(i * chunk, chunk)
        return step(
            kv_ref[0, 0, pl.ds(at, chunk), :width],
            kv_ref[0, 0, pl.ds(at, chunk), width:],
            None,
            carry,
        )

    full = valid // chunk

    def tail_step(_, carry):
        at = pl.multiple_of(full * chunk, chunk)
        place = at + lax.broadcasted_iota(jnp.int32, (1, chunk), 1)
        return step(
            kv_ref[0, 0, pl.ds(at, chunk), :width],
            kv_ref[0, 0, pl.ds(at, chunk), width:],
            jnp.where(place < valid, 0.0, MASKED),
            carry,
        )

    carry = (
        jnp.full((rows, 1), MASKED, jnp.float32),
        jnp.zeros((rows, 1), jnp.float32),
        jnp.zeros((rows, width), jnp.float32),
    )
    carry = lax.fori_loop(0, full, full_step, carry)
    carry = lax.fori_loop(0, jnp.where(valid > full * chunk, 1, 0), tail_step, carry)
    carry = lax.fori_loop(
        0, own, lambda _, c: step(own_k[...], own_v[...], None, c), carry
    )
    peak, mass, total = carry
    some = mass > 0.0
    safe = jnp.where(some, mass, 1.0)
    out_ref[:, pl.ds(pl.multiple_of(head * width, width), width)] = (total / safe).astype(
        jnp.bfloat16
    )
    level = jnp.where(some, peak * to_log2 + jnp.log2(safe), MASKED)
    first = level.astype(jnp.bfloat16).astype(jnp.float32)
    second = (level - first).astype(jnp.bfloat16).astype(jnp.float32)
    third = level - first - second
    lane = lax.broadcasted_iota(jnp.int32, (rows, width), 1)
    before = jnp.where(head == 0, 0.0, out_ref[:, heads * width :].astype(jnp.float32))
    marks = jnp.where(lane == 3 * head, first, before)
    marks = jnp.where(lane == 3 * head + 1, second, marks)
    marks = jnp.where(lane == 3 * head + 2, third, marks)
    out_ref[:, heads * width :] = marks.astype(jnp.bfloat16)


def attend(meta, queries, cache_t, packed, seqs, heads, width):
    rows = queries.shape[0] // seqs
    block = math.gcd(rows, 512)
    blocks = rows // block
    cache_rows = cache_t.shape[2]
    own_rows = packed.shape[0]
    chunk = math.gcd(cache_rows, 1024)
    keys = cache_rows + own_rows
    return pl.pallas_call(
        functools.partial(attention_kernel, seqs, heads, chunk),
        grid_spec=pltpu.PrefetchScalarGridSpec(
            num_scalar_prefetch=1,
            grid=(seqs, blocks, heads),
            in_specs=[
                pl.BlockSpec((block, width), lambda s, b, h, m: (s * blocks + b, h)),
                pl.BlockSpec((1, 1, cache_rows, 2 * width), lambda s, b, h, m: (s, h, 0, 0)),
                pl.BlockSpec((own_rows, width), lambda s, b, h, m: (0, 3 * h + 1)),
                pl.BlockSpec((own_rows, width), lambda s, b, h, m: (0, 3 * h + 2)),
            ],
            out_specs=pl.BlockSpec(
                (block, (heads + 1) * width), lambda s, b, h, m: (s * blocks + b, 0)
            ),
        ),
        out_shape=jax.ShapeDtypeStruct((seqs * rows, (heads + 1) * width), jnp.bfloat16),
        compiler_params=pltpu.CompilerParams(vmem_limit_bytes=44 << 20),
        cost_estimate=pl.CostEstimate(
            flops=8 * seqs * rows * heads * keys * width,
            bytes_accessed=2 * seqs * heads * (2 * keys * width + 2 * rows * width),
            transcendentals=seqs * rows * heads * keys,
        ),
    )(meta, queries, cache_t, packed, packed)


def per_device(
    kv_size, hidden_in, gain_attn, w_qkv, cache_kv, cache_len, w_out, gain_mlp, w_gate_up, w_down
):
    heads = w_qkv.shape[1]
    width = w_qkv.shape[2] // 3
    own_rows = hidden_in.shape[0]
    half_rows = own_rows // PARTS
    seqs, cache_rows = cache_kv.shape[0], cache_kv.shape[1]
    kv_index = lax.axis_index("kv")
    model = hidden_in.shape[1]

    def swap(array, bit):
        return lax.ppermute(array, "kv", [(i, i ^ bit) for i in range(kv_size)])

    bits = [1 << i for i in range(kv_size.bit_length() - 1)][::-1]
    order = [0]
    gate_up_set, down_set = [w_gate_up], [w_down]
    for level, bit in enumerate(bits):
        gate_up_set = gate_up_set + [swap(w, bit) for w in gate_up_set]
        down_set = down_set + [swap(w, bit) for w in down_set]
        order = order + [o ^ bit for o in order]

    inputs = [hidden_in[p * half_rows : (p + 1) * half_rows] for p in range(PARTS)]
    flat_qkv = w_qkv.reshape(model, heads * 3 * width)
    cache_t = cache_kv.transpose(0, 2, 1, 3)
    packed_parts, query_parts = [], []
    for part in inputs:
        block_input = lax.all_gather(part, "tp", axis=0, tiled=True)
        normed = rms_scale(block_input, gain_attn)
        packed = jnp.dot(normed, flat_qkv, preferred_element_type=jnp.float32)
        packed = packed.astype(jnp.bfloat16)
        packed_parts.append(packed)
        query_mine = jnp.concatenate(
            [packed[:, 3 * h * width : (3 * h + 1) * width] for h in range(heads)], axis=1
        )
        query_parts.append(lax.all_gather(query_mine, "kv", axis=0, tiled=True))
    packed_all = jnp.concatenate(packed_parts, axis=0)

    valid = jnp.clip(cache_len - kv_index * cache_rows, 0, cache_rows)
    own_seq = kv_index * seqs // kv_size
    own = (jnp.arange(seqs, dtype=jnp.int32) == own_seq).astype(jnp.int32)
    meta = jnp.concatenate([valid.astype(jnp.int32), own])

    residuals, mlp_parts = [], []
    for part, queries in zip(inputs, query_parts):
        partial = attend(meta, queries, cache_t, packed_all, seqs, heads, width)
        partial = partial.reshape(kv_size, queries.shape[0] // kv_size, (heads + 1) * width)
        parts = lax.all_to_all(partial, "kv", split_axis=0, concat_axis=0, tiled=True)
        marks = parts[:, :, heads * width : heads * width + 3 * heads].astype(jnp.float32)
        level = marks.reshape(kv_size, -1, heads, 3).sum(axis=3)
        scaling = jnp.exp2(level - jnp.max(level, axis=0, keepdims=True))
        scaling = scaling / jnp.sum(scaling, axis=0, keepdims=True)
        attended = jnp.concatenate(
            [
                jnp.sum(
                    parts[:, :, h * width : (h + 1) * width].astype(jnp.float32)
                    * scaling[:, :, h : h + 1],
                    axis=0,
                )
                for h in range(heads)
            ],
            axis=1,
        ).astype(jnp.bfloat16)
        terms = jnp.dot(attended, w_out, preferred_element_type=jnp.float32)
        terms = terms.astype(jnp.bfloat16)
        heads_sum = lax.psum_scatter(terms, "tp", scatter_dimension=0, tiled=True)
        residual = part.astype(jnp.float32) + heads_sum.astype(jnp.float32)
        residuals.append(residual)
        mlp_parts.append(
            lax.all_gather(rms_scale(residual, gain_mlp), "tp", axis=0, tiled=True)
        )

    depth = model // kv_size
    outs = []
    for residual, mlp_in in zip(residuals, mlp_parts):
        gate_up = 0.0
        for code, w in zip(order, gate_up_set):
            piece = lax.dynamic_slice_in_dim(mlp_in, (kv_index ^ code) * depth, depth, 1)
            gate_up = gate_up + jnp.einsum(
                "td,dgf->tgf", piece, w, preferred_element_type=jnp.float32
            )
        activated = (jax.nn.silu(gate_up[:, 0, :]) * gate_up[:, 1, :]).astype(jnp.bfloat16)
        terms = jnp.concatenate(
            [
                jnp.dot(activated, w, preferred_element_type=jnp.float32).astype(jnp.bfloat16)
                for w in down_set
            ],
            axis=1,
        )
        down_own = lax.psum_scatter(terms, "tp", scatter_dimension=0, tiled=True)
        blocks = [down_own[:, i * depth : (i + 1) * depth] for i in range(kv_size)]
        for level, bit in enumerate(bits[::-1]):
            flip = (kv_index & bit) != 0
            stride = kv_size >> (level + 1)
            blocks = [jnp.where(flip, blocks[i ^ stride], blocks[i]) for i in range(kv_size)]
        in_place = [None] * kv_size
        for position, code in enumerate(order):
            in_place[code] = blocks[position]
        outs.append(residual + jnp.concatenate(in_place, axis=1).astype(jnp.float32))
    return jnp.concatenate(outs, axis=0).astype(jnp.bfloat16)


def solution(mesh):
    in_specs = (
        P(("kv", "tp"), None),
        P(),
        P(None, "tp", None),
        P(None, "kv", "tp", None),
        P(),
        P("tp", None),
        P(),
        P("kv", None, "tp"),
        P("tp", "kv"),
    )
    out_specs = P(("kv", "tp"), None)
    body = functools.partial(per_device, mesh.shape["kv"])

    return jax.shard_map(body, mesh=mesh, in_specs=in_specs, out_specs=out_specs, check_vma=False)
```

time: 835 us -> 552 us (0.66)
  waiting for transfers between devices: 541 us -> 350 us
  other arithmetic: 84.6 us -> 13.3 us
  matrix products: 124 us -> 56.5 us
  Pallas kernels: 0 us -> 54.2 us
  blocking collectives: 0 us -> 34.9 us
  local copies, waits for them, and re-layouts: 52.2 us -> 27.5 us
  starting transfers between devices: 12.1 us -> 1.32 us
    all_gather x4 -> x3, waiting for transfers between devices: 253 us -> 78.4 us  [the longest x1 65.1 us: per_device(): block_input = lax.all_gather(part, 'tp', axis=0, tiled=True)]
    psum x1 -> x0, waiting for transfers between devices: 155 us -> none  [per_device(): lax.psum(jnp.dot(attended, w_out, preferred_element_type=jnp.float32).ast...]
    ppermute x0 -> x6, waiting for transfers between devices: none -> 94.3 us  [swap(): return lax.ppermute(array, 'kv', [(i, i ^ bit) for i in range(kv_size)])]
    reduce_scatter x1 -> x2, waiting for transfers between devices: 88.4 us -> 177 us  [the longest x1 88.7 us: per_device(): down_own = lax.psum_scatter(terms, 'tp', scatter_dimension=0, tiled=True)]
    dot_general x8 -> x10, matrix products: 124 us -> 56.5 us  [the longest x4 27.2 us: per_device(): jnp.einsum('td,dgf->tgf', piece, w, preferred_element_type=jnp.float32)]
    pallas_call x0 -> x1, Pallas kernels: none -> 54.2 us  [attend(): pl.pallas_call(functools.partial(attention_kernel, seqs, heads, chunk), g...]
    reduce_sum x4 -> x2, other arithmetic: 43.5 us -> 0.46 us  [the longest x1 0.43 us: per_device(): jnp.sum(parts[:, :, h * width:(h + 1) * width].astype(jnp.float32) * scal...]
    all_to_all x3 -> x0, waiting for transfers between devices: 42.2 us -> none  [the longest x1 42.2 us: per_device(): lax.all_to_all(accum_all[None], 'kv', split_axis=1, concat_axis=0, tiled=...]
  transfers between devices with their start and end apart: 9 -> 11, of which waited for: 7 -> 6; matrix products, arithmetic and copies ran while one was open for 11% -> 11% of each run, Pallas kernels for 0% -> 0%
where the time goes in v1:
time: 552 us; the launch traced here: 551 us
  waiting for transfers between devices  350 us (63%)
  matrix products  56.5 us (10%)
  Pallas kernels  54.2 us (10%)
  blocking collectives  34.9 us (6%)
  local copies, waits for them, and re-layouts  27.5 us (5%)
  between operations  13.4 us (2%)
  other arithmetic  13.3 us (2%)
    ppermute x6, waiting for transfers between devices, swap(): return lax.ppermute(array, 'kv', [(i, i ^ bit) for i in range(kv_size)])  94.3 us
    reduce_scatter x1, waiting for transfers between devices, per_device(): down_own = lax.psum_scatter(terms, 'tp', scatter_dimension=0, tiled=True)  88.7 us
    reduce_scatter x1, waiting for transfers between devices, per_device(): heads_sum = lax.psum_scatter(terms, 'tp', scatter_dimension=0, tiled=True)  88 us
    all_gather x1, waiting for transfers between devices, per_device(): block_input = lax.all_gather(part, 'tp', axis=0, tiled=True)  65.1 us
    pallas_call x1, Pallas kernels, attend(): pl.pallas_call(functools.partial(attention_kernel, seqs, heads, chunk), g...  54.2 us
    all_to_all x1, blocking collectives, per_device(): lax.all_to_all(partial, 'kv', split_axis=0, concat_axis=0, tiled=True)  34.9 us
    dot_general x4, matrix products, per_device(): jnp.einsum('td,dgf->tgf', piece, w, preferred_element_type=jnp.float32)  27.2 us
    unnamed x24, local copies, waits for them, and re-layouts  24.8 us
  transfers between devices with their start and end apart: 11, of which 6 were waited for; matrix products, arithmetic and copies ran while one was open for 11% of the time, Pallas kernels for 0%

profile of v1, /device:TPU:0, one launch (start us, length us, event | category | flops | bytes accessed | tf_op | source)
XLA Modules:
  0.0 551.2 jit_solution(11823056953602941320)
XLA Ops:
  7.3 12.6 %copy.24 = bf16[512,8,4,384]{3,1,2,0:T(8,128)(2,1)} copy(bf16[512,8,4,384]{3,2,1,0:T(4,128)(2,1)} %bitcast.53) | data formatting | bytes 25165824
  19.9 65.1 %all-gather.4.cloned.1.call-done = bf16[512,4096]{1,0:T(8,128)(2,1)} async-done(((bf16[64,4096]{1,0:T(8,128)(2,1)}), bf16[512,4096]{1,0:T(8,128)(2,1)}) %all-gather.4.cloned.1.call-update) | async-done | bytes 4194320 | tf_op jit(solution)/shard_map/all_gather | solution.py:156
  85.0 3.2 fusion.1
  88.5 9.8 %fusion.8.own_k.own_v = bf16[512,1536]{1,0:T(8,128)(2,1)S(1)} fusion(bf16[4096,1536]{1,0:T(8,128)(2,1)} %bitcast.54, bf16[512,4096]{1,0:T(8,128)(2,1)S(1)} %copy-done.5, f32[4096]{0:T(1024)S(1)} %copy-done.9, f32[512]{0:T(512)S(1)} %add_rsqrt_fusion), kind=kOutput, calls=%fused_computation.13 | convolution fusion | flops 6451625984 | bytes 18368512 | tf_op jit(solution)/shard_map/dot_general | solution.py:158
  98.4 1.1 copy-done
  99.6 0.9 pad_maximum_fusion.1
  100.5 7.8 %copy.26 = bf16[2,2048,4,256]{3,1,2,0:T(8,128)(2,1)} copy(bf16[2,2048,4,256]{3,2,1,0:T(4,128)(2,1)} %param.12) | data formatting | bytes 16777216 | tf_op args[3]
  108.4 13.3 %all-gather.6.cloned.1.call-done.q_ref = bf16[2048,512]{1,0:T(8,128)(2,1)} async-done(((bf16[512,512]{1,0:T(8,128)(2,1)}), bf16[2048,512]{1,0:T(8,128)(2,1)}) %all-gather.6.cloned.1.call-update) | async-done | bytes 2097168 | tf_op jit(solution)/shard_map/all_gather | solution.py:164
  121.7 1.4 copy-done.1
  123.1 1.6 copy-done.2
  124.7 54.2 %shard_map.91 = bf16[2048,640]{1,0:T(8,128)(2,1)S(1)} custom-call(s32[4]{0:T(128)S(1)} %pad_add_fusion.meta, bf16[2048,512]{1,0:T(8,128)(2,1)S(1)} %copy-done.2, bf16[2,4,2048,256]{3,2,1,0:T(8,128)(2,1)} %bitcast.55, bf16[512,1536]{1,0:T(8,128)(2,1)S(1)} %copy-done.1, bf16[512,1536]{1,0:T(8,128)(2,1)S(1)} %copy-done.1), custom_call_target="tpu_custom_call" | custom-call | flops 21474836480 | bytes 14680064 | tf_op jit(solution)/shard_map/pallas_call | solution.py:104
  179.0 2.6 copy.14
  181.6 34.9 %all_to_all.5 = bf16[4,512,640]{1,2,0:T(8,128)(2,1)S(1)} all-to-all(bf16[4,512,640]{1,2,0:T(8,128)(2,1)} %copy.14), channel_id=1, replica_groups=mesh['tp'=8,'kv'=4] {'kv'}, dimensions={0} | all-to-all | bytes 5242880 | tf_op jit(solution)/shard_map/all_to_all | solution.py:176
  217.1 6.6 %convolution_convert_fusion = bf16[512,4096]{1,0:T(8,128)(2,1)} fusion(bf16[512,4096]{1,0:T(8,128)(2,1)} %param.14, bf16[512,128]{0,1:T(8,128)(2,1)S(1)} %get-tuple-element.6, bf16[512,128]{0,1:T(8,128)(2,1)S(1)} %get-tuple-element.7, bf16[512,128]{0,1:T(8,128)(2,1)S(1)} %get-tuple-element.8, bf16[512,128]{0,1:T(8,128)(2,1)S(1)} %get-tuple-element.5), kind=kOutput, calls=%fused_computation.7 | convolution fusion | flops 2151677952 | bytes 8912896 | tf_op jit(solution)/shard_map/dot_general | solution.py:192
  224.3 88.0 %reduce-scatter.3.cloned.1.call-done = bf16[64,4096]{1,0:T(8,128)(2,1)} async-done(((bf16[512,4096]{1,0:T(8,128)(2,1)}), bf16[64,4096]{1,0:T(8,128)(2,1)}) %reduce-scatter.3.cloned.1.call-update) | async-done | bytes 524304 | tf_op jit(solution)/shard_map/reduce_scatter | solution.py:194
  312.2 1.3 multiply_reduce_fusion
  313.6 2.0 multiply_convert_fusion
  315.8 31.3 %collective-permute-done = bf16[1024,2,1376]{0,2,1:T(8,128)(2,1)} collective-permute-done((bf16[1024,2,1376]{0,2,1:T(8,128)(2,1)}, bf16[1024,2,1376]{0,2,1:T(8,128)(2,1)}, u32[]{:S(2)}, u32[]{:S(2)}) %collective-permute-start) | collective-permute-done | bytes 5636128 | tf_op jit(solution)/shard_map/ppermute | solution.py:141
  347.7 63.0 %collective-permute-done.3 = bf16[1376,1024]{1,0:T(8,128)(2,1)} collective-permute-done((bf16[1376,1024]{1,0:T(8,128)(2,1)S(1)}, bf16[1376,1024]{1,0:T(8,128)(2,1)}, u32[]{:S(2)}, u32[]{:S(2)}) %collective-permute-start.3) | collective-permute-done | bytes 2818080 | tf_op jit(solution)/shard_map/ppermute | solution.py:141
  410.7 5.6 %fusion.19 = f32[512,2,1376]{0,2,1:T(8,128)S(1)} fusion(bf16[1024,2,1376]{0,2,1:T(8,128)(2,1)} %collective-permute-done, bf16[512,4096]{1,0:T(8,128)(2,1)} %all-gather.8.cloned.1.call-done, s32[]{:T(128)S(6)} %select_n.59), kind=kOutput, calls=%fused_computation.28 | convolution fusion | flops 2885681152 | bytes 12320772 | tf_op jit(solution)/shard_map/td,dgf->tgf/dot_general | solution.py:207
  416.3 5.3 fusion.21
  421.6 7.6 %fusion.17 = f32[512,2,1376]{0,2,1:T(8,128)} fusion(bf16[1024,2,1376]{0,2,1:T(8,128)(2,1)} %collective-permute-done.1, bf16[512,4096]{1,0:T(8,128)(2,1)S(1)} %copy-done.6, s32[]{:T(128)S(6)} %select_n.60), kind=kOutput, calls=%fused_computation.26 | convolution fusion | flops 2885681152 | bytes 12320772 | tf_op jit(solution)/shard_map/td,dgf->tgf/dot_general | solution.py:207
  429.2 8.7 %add_add_fusion = f32[512,2,1376]{0,2,1:T(8,128)S(1)} fusion(f32[512,2,1376]{0,2,1:T(8,128)} %fusion.17, f32[512,2,1376]{0,2,1:T(8,128)S(1)} %fusion.21, f32[512,2,1376]{0,2,1:T(8,128)S(1)} %fusion.19, bf16[1024,2,1376]{0,2,1:T(8,128)(2,1)} %collective-permute-done.2, bf16[512,4096]{1,0:T(8,128)(2,1)} %all-gather.8.cloned.1.call-done, s32[]{:T(128)S(6)} %select_n.61), kind=kOutput, calls=%fused_computation.8 | convolution fusion | flops 2889908224 | bytes 29229060 | tf_op jit(solution)/shard_map/td,dgf->tgf/dot_general | solution.py:207
  438.0 1.0 fusion.12
  438.9 1.8 convolution_convert_fusion.4
  440.8 3.6 convolution_convert_fusion.3
  444.4 3.6 convolution_convert_fusion.1
  448.1 3.6 convolution_convert_fusion.2
  451.7 2.1 pad_maximum_fusion
  453.9 88.7 %reduce-scatter.5.cloned.1.call-done = bf16[64,4096]{1,0:T(8,128)(2,1)} async-done(((bf16[512,4096]{1,0:T(8,128)(2,1)}), bf16[64,4096]{1,0:T(8,128)(2,1)}) %reduce-scatter.5.cloned.1.call-update) | async-done | bytes 524304 | tf_op jit(solution)/shard_map/reduce_scatter | solution.py:218
  542.6 1.1 broadcast_select_fusion.7
  543.7 1.0 add_convert_fusion
  (53 shorter events, 3.1 us)
Async XLA Ops:
  6.5 78.5 %all-gather.4.cloned.1.call-start = ((), (), s32[]{:S(2)}) async-start(), calls=%async_computation.3 | async-start | bytes 4718592 | tf_op jit(solution)/shard_map/all_gather | solution.py:156
  7.3 114.4 %all-gather.6.cloned.1.call-start = ((), (), s32[]{:S(2)}) async-start(), calls=%async_computation.4 | async-start | bytes 2621440 | tf_op jit(solution)/shard_map/all_gather | solution.py:164
  7.3 80.9 %copy-start.9 = (f32[4096]{0:T(1024)S(1)}, f32[4096]{0:T(1024)}, u32[]{:S(2)}) copy-start(f32[4096]{0:T(1024)} %param.10) | copy-start | bytes 49156
  85.0 3.4 copy-start.5
  98.4 1.1 copy-start
  100.4 211.8 %reduce-scatter.3.cloned.1.call-start = ((), (), s32[]{:S(2)}) async-start(), calls=%async_computation.5 | async-start | bytes 4718592 | tf_op jit(solution)/shard_map/reduce_scatter | solution.py:194
  100.5 7.8 %copy-start.10 = (s32[2]{0:T(128)S(1)}, s32[2]{0:T(128)}, u32[]{:S(2)}) copy-start(s32[2]{0:T(128)} %param.13) | copy-start | bytes 28
  121.7 1.4 copy-start.1
  123.1 1.6 copy-start.2
  223.7 88.5 %copy-start.3 = (bf16[64,4096]{1,0:T(8,128)(2,1)S(1)}, bf16[64,4096]{1,0:T(8,128)(2,1)}, u32[]{:S(2)}) copy-start(bf16[64,4096]{1,0:T(8,128)(2,1)} %param.9) | copy-start | bytes 1572868
  223.8 89.8 %copy-start.7 = (f32[4096]{0:T(1024)S(1)}, f32[4096]{0:T(1024)}, u32[]{:S(2)}) copy-start(f32[4096]{0:T(1024)} %param.15) | copy-start | bytes 49156
  223.8 123.3 %copy-start.8 = (bf16[1376,1024]{1,0:T(8,128)(2,1)S(1)}, bf16[1376,1024]{1,0:T(8,128)(2,1)}, u32[]{:S(2)}) copy-start(bf16[1376,1024]{1,0:T(8,128)(2,1)} %param.17) | copy-start | bytes 8454148
  223.8 186.9 %all-gather.8.cloned.1.call-start = ((), (), s32[]{:S(2)}) async-start(), calls=%async_computation.6 | async-start | bytes 4718592 | tf_op jit(solution)/shard_map/all_gather | solution.py:198
  223.8 123.2 %collective-permute-start = (bf16[1024,2,1376]{0,2,1:T(8,128)(2,1)}, bf16[1024,2,1376]{0,2,1:T(8,128)(2,1)}, u32[]{:S(2)}, u32[]{:S(2)}) collective-permute-start(bf16[1024,2,1376]{0,2,1:T(8,128)(2,1)} %param.16), channel_id=1, source_target_pairs={{0,2},{1,3},{2,0},{3,1},{4,6},{5,7},{6,4},{7,5},{8,10},{9,11},{10,... | collective-permute-start | bytes 16908296 | tf_op jit(solution)/shard_map/ppermute | solution.py:141
  315.7 226.9 %reduce-scatter.5.cloned.1.call-start = ((), (), s32[]{:S(2)}) async-start(), calls=%async_computation.7 | async-start | bytes 4718592 | tf_op jit(solution)/shard_map/reduce_scatter | solution.py:218
  315.7 105.9 %collective-permute-start.1 = (bf16[1024,2,1376]{0,2,1:T(8,128)(2,1)}, bf16[1024,2,1376]{0,2,1:T(8,128)(2,1)}, u32[]{:S(2)}, u32[]{:S(2)}) collective-permute-start(bf16[1024,2,1376]{0,2,1:T(8,128)(2,1)} %param.16), channel_id=1, source_target_pairs={{0,1},{1,0},{2,3},{3,2},{4,5},{5,4},{6,7},{7,6},{8,9},{9,8},{10,11... | collective-permute-start | bytes 16908296 | tf_op jit(solution)/shard_map/ppermute | solution.py:141
  347.1 82.2 %collective-permute-start.2 = (bf16[1024,2,1376]{0,2,1:T(8,128)(2,1)}, bf16[1024,2,1376]{0,2,1:T(8,128)(2,1)}, u32[]{:S(2)}, u32[]{:S(2)}) collective-permute-start(bf16[1024,2,1376]{0,2,1:T(8,128)(2,1)} %collective-permute-done), channel_id=1, source_target_pairs={{0,1},{1,0},{2,3},{3,2},{4,5},{5,4},{6,7},{7,6},{8,9},{9,8},{10,11... | collective-permute-start | bytes 16908296 | tf_op jit(solution)/shard_map/ppermute | solution.py:141
  347.1 63.6 %collective-permute-start.3 = (bf16[1376,1024]{1,0:T(8,128)(2,1)S(1)}, bf16[1376,1024]{1,0:T(8,128)(2,1)}, u32[]{:S(2)}, u32[]{:S(2)}) collective-permute-start(bf16[1376,1024]{1,0:T(8,128)(2,1)S(1)} %copy-done.8), channel_id=1, source_target_pairs={{0,2},{1,3},{2,0},{3,1},{4,6},{5,7},{6,4},{7,5},{8,10},{9,11},{10,... | collective-permute-start | bytes 8454152 | tf_op jit(solution)/shard_map/ppermute | solution.py:141
  347.5 100.6 %collective-permute-start.4 = (bf16[1376,1024]{1,0:T(8,128)(2,1)S(1)}, bf16[1376,1024]{1,0:T(8,128)(2,1)}, u32[]{:S(2)}, u32[]{:S(2)}) collective-permute-start(bf16[1376,1024]{1,0:T(8,128)(2,1)S(1)} %copy-done.8), channel_id=1, source_target_pairs={{0,1},{1,0},{2,3},{3,2},{4,5},{5,4},{6,7},{7,6},{8,9},{9,8},{10,11... | collective-permute-start | bytes 8454152 | tf_op jit(solution)/shard_map/ppermute | solution.py:141
  410.7 33.8 %collective-permute-start.5 = (bf16[1376,1024]{1,0:T(8,128)(2,1)}, bf16[1376,1024]{1,0:T(8,128)(2,1)}, u32[]{:S(2)}, u32[]{:S(2)}) collective-permute-start(bf16[1376,1024]{1,0:T(8,128)(2,1)} %collective-permute-done.3), channel_id=1, source_target_pairs={{0,1},{1,0},{2,3},{3,2},{4,5},{5,4},{6,7},{7,6},{8,9},{9,8},{10,11... | collective-permute-start | bytes 8454152 | tf_op jit(solution)/shard_map/ppermute | solution.py:141
  410.7 5.6 %copy-start.6 = (bf16[512,4096]{1,0:T(8,128)(2,1)S(1)}, bf16[512,4096]{1,0:T(8,128)(2,1)}, u32[]{:S(2)}) copy-start(bf16[512,4096]{1,0:T(8,128)(2,1)} %all-gather.8.cloned.1.call-done) | copy-start | bytes 12582916
  453.9 89.8 %copy-start.4 = (bf16[64,4096]{1,0:T(8,128)(2,1)S(1)}, bf16[64,4096]{1,0:T(8,128)(2,1)}, u32[]{:S(2)}) copy-start(bf16[64,4096]{1,0:T(8,128)(2,1)} %reduce-scatter.3.cloned.1.call-done) | copy-start | bytes 1572868
Sparse Core Ops, SparseCore 0:
  9.5 75.5 all-gather.3
  100.6 21.0 all-gather.5
  223.9 88.2 reduce-scatter.2
  315.8 72.4 all-gather.7
  454.0 88.4 reduce-scatter.4
